TPU v7x, 32 devices: a whole 2x2x4 slice. The times are simulated.
32 devices in a mesh: section: 4 (over z), tp: 8 (over y, x, core).
Axes of the slice: x: 2, y: 2, z: 4, core: 2. Of those that a mesh axis runs over, the one named last changes fastest.
Arguments:
- latents: bfloat16 [1024, 8, 2048], P('tp', 'section'), may hold values from -6 to 6
- timestep: int32 [8], replicated, may hold values from 0 to 999
- target: int32 [8], replicated, may hold values from 0 to 3, as said below
- qkv_weight: bfloat16 [4, 2048, 3, 2048], P('section', None, None, 'tp'), may hold values from -0.125 to 0.125
- mod_weight: bfloat16 [4, 256, 3, 2048], P('section'), may hold values from -2.6 to 2.6
- out_weight: bfloat16 [4, 2048, 2048], P('section', 'tp'), may hold values from -0.125 to 0.125
Outputs:
- updated: bfloat16 [1024, 8, 2048], P('tp', 'section')
Inputs may be any that keep to these rules, and one draw needn't show every extreme that they name: target[l] is l // 2 or l // 2 + 1; of one section's 2 latents at most 1 name the next section, exactly 1 for section 0, none for the last section.
All inputs are finite; a program needn't handle non-finite values.
Results may differ from a plain program's by a relative error of at most 0.023.
Values may be sent and summed in bfloat16 or wider, within the bound.
A program may use at most 128 MiB of HBM per device.

v0:
```python
import functools
import math

import jax
import jax.numpy as jnp
from jax import lax
from jax.experimental import pallas as pl
from jax.experimental.pallas import tpu as pltpu
from jax.sharding import PartitionSpec as P

HEAD_DIM = 128
FREQ = 256
MOVE_MAX = 1


def from_behind(shard, axis, by):
    peers = lax.axis_size(axis)
    pairs = [(i, i + by) for i in range(peers) if 0 <= i + by < peers]
    return lax.ppermute(shard, axis, pairs)


def time_embed(steps):
    half_width = FREQ // 2
    frequency = jnp.exp(-math.log(10000.0) * jnp.arange(half_width, dtype=jnp.float32) / half_width)
    angles = steps.astype(jnp.float32)[:, None] * frequency[None, :]
    return jnp.concatenate([jnp.cos(angles), jnp.sin(angles)], axis=1)


def modulate(steps, mod_table):
    feature = jax.nn.silu(time_embed(steps))
    return jnp.einsum(
        "bf,fcd->bcd", feature, mod_table.astype(jnp.float32), precision=lax.Precision.HIGHEST
    )


def normalize(values, shift, scale):
    row_mean = jnp.mean(values, axis=-1, keepdims=True)
    centred = values - row_mean
    variance = jnp.mean(centred * centred, axis=-1, keepdims=True)
    return centred * lax.rsqrt(variance + 1e-06) * (1.0 + scale) + shift


def expert_block(batch, steps, qkv_local, mod_table, out_local):
    mods = modulate(steps, mod_table)
    values = batch.astype(jnp.float32)
    hidden = normalize(values, mods[None, :, 0], mods[None, :, 1]).astype(jnp.bfloat16)
    packed = jnp.einsum(
        "sbd,dce->sbce",
        lax.all_gather(hidden, "tp", axis=0, tiled=True),
        qkv_local,
        preferred_element_type=jnp.float32,
    ).astype(jnp.bfloat16)
    tok_all = packed.shape[0]
    slot_count = packed.shape[1]
    local_width = packed.shape[3]
    head_local = local_width // HEAD_DIM
    split_heads = packed.reshape(tok_all, slot_count, 3, head_local, HEAD_DIM)
    query = split_heads[:, :, 0]
    keys_now = split_heads[:, :, 1]
    vals_now = split_heads[:, :, 2]
    scores = jnp.einsum(
        "qbhe,kbhe->bhqk", query, keys_now, preferred_element_type=jnp.float32
    ) * HEAD_DIM ** (-0.5)
    soft = jax.nn.softmax(scores, axis=-1).astype(jnp.bfloat16)
    mixed = jnp.einsum("bhqk,kbhe->qbhe", soft, vals_now, preferred_element_type=jnp.float32)
    mixed = mixed.astype(jnp.bfloat16).reshape(tok_all, slot_count, local_width)
    proj = lax.psum_scatter(
        jnp.einsum("sbk,kd->sbd", mixed, out_local, preferred_element_type=jnp.float32).astype(
            jnp.bfloat16
        ),
        "tp",
        scatter_dimension=0,
        tiled=True,
    ).astype(jnp.float32)
    return (values + mods[None, :, 2] * proj).astype(jnp.bfloat16)


def movers_first(move_flags, slots):
    order_keys = jnp.where(move_flags, 0, 1).astype(jnp.int32) * slots + jnp.arange(
        slots, dtype=jnp.int32
    )
    return jnp.argsort(order_keys)[:MOVE_MAX]


def body(latents, timestep, target, qkv_weight, mod_weight, out_weight):
    slots = latents.shape[1]
    home_section = lax.axis_index("section")
    prev_section = jnp.maximum(home_section - 1, 0)
    own_steps = lax.dynamic_slice_in_dim(timestep, home_section * slots, slots)
    own_target = lax.dynamic_slice_in_dim(target, home_section * slots, slots)
    prev_steps = lax.dynamic_slice_in_dim(timestep, prev_section * slots, slots)
    prev_target = lax.dynamic_slice_in_dim(target, prev_section * slots, slots)
    own_move = own_target != home_section
    prev_move = prev_target == home_section
    qkv_local = qkv_weight[0]
    mod_table = mod_weight[0]
    out_local = out_weight[0]
    own_order = movers_first(own_move, slots)
    prev_order = movers_first(prev_move, slots)
    outgoing = jnp.take(latents, own_order, axis=1)
    incoming = from_behind(outgoing, "section", 1)
    batch = jnp.concatenate([latents, incoming], axis=1)
    steps = jnp.concatenate([own_steps, jnp.take(prev_steps, prev_order, axis=0)], axis=0)
    result = expert_block(batch, steps, qkv_local, mod_table, out_local)
    coming_back = from_behind(result[:, slots:], "section", -1)
    placing = own_order[None, :] == jnp.arange(slots, dtype=jnp.int32)[:, None]
    returned = jnp.einsum(
        "lm,sme->sle", placing.astype(jnp.bfloat16), coming_back, preferred_element_type=jnp.float32
    ).astype(jnp.bfloat16)
    return jnp.where(own_move[None, :, None], returned, result[:, :slots])


MESH = pl.DeviceIdType.MESH
F32 = jnp.float32
BF16 = jnp.bfloat16
CHUNKS = 4


def block_kernel(
    sections, target, latents, mods, w_qkv_hbm, w_out_hbm,
    updated,
    outgoing, gathered, w_out, w_qkv, qkv, mix_send, mix_recv, raw, back, back_in,
    load_sem, send_sem, recv_sem, mix_send_sem, mix_recv_sem, hand_sem, back_sem,
):
    tok, width = raw.shape
    slots = latents.shape[1] // width
    local = w_out.shape[2]
    heads = local // HEAD_DIM
    peers = gathered.shape[1]
    cols = width // CHUNKS
    section = lax.axis_index("section")
    me = lax.axis_index("tp")
    core = me % 2
    x = (me // 2) % 2
    y = me // 4
    to_x = 2 - 4 * x
    to_y = 4 - 8 * y
    to_c = 1 - 2 * core
    dev_x, dev_y, dev_c = me + to_x, me + to_y, me + to_c
    has_prev = section > 0
    has_next = section < sections - 1

    load_qkv = pltpu.make_async_copy(w_qkv_hbm, w_qkv, load_sem.at[CHUNKS])
    load_out = [
        pltpu.make_async_copy(
            w_out_hbm.at[:, j * cols : (j + 1) * cols], w_out.at[j, me], load_sem.at[j]
        )
        for j in range(CHUNKS)
    ]
    for copy in load_out:
        copy.start()
    load_qkv.start()

    barrier = pltpu.get_barrier_semaphore()
    for step in range(1, peers):
        pl.semaphore_signal(
            barrier, inc=1, device_id=(section, (me + step) % peers), device_id_type=MESH
        )

    @pl.when(has_prev)
    def _():
        pl.semaphore_signal(barrier, inc=1, device_id=(section - 1, me), device_id_type=MESH)

    @pl.when(has_next)
    def _():
        pl.semaphore_signal(barrier, inc=1, device_id=(section + 1, me), device_id_type=MESH)

    beside = jnp.minimum(section, 1) + jnp.minimum(sections - 1 - section, 1)
    pl.semaphore_wait(barrier, peers - 1 + beside)

    def hand_copy():
        return pltpu.make_async_remote_copy(
            outgoing, raw, hand_sem.at[0], hand_sem.at[1],
            device_id=(section + 1, me), device_id_type=MESH,
        )

    def back_copy(j):
        return pltpu.make_async_remote_copy(
            back.at[j], back_in.at[j], back_sem.at[0, j], back_sem.at[1, j],
            device_id=(section - 1, me), device_id_type=MESH,
        )

    moves = [
        jnp.broadcast_to((target[section * slots + j] != section).astype(jnp.int32), (16, width)) != 0
        for j in range(slots)
    ]

    def choose(i, _):
        rows = pl.ds(pl.multiple_of(i * 16, 16), 16)
        outgoing[rows, :] = jnp.where(moves[0], latents[rows, :width], latents[rows, width:])
        return 0

    lax.fori_loop(0, tok // 16, choose, 0)

    @pl.when(has_next)
    def _():
        hand_copy().start()

    def piece(item, owner, part):
        kind, j = item
        ref = w_out if kind == "w" else gathered
        rows = ref.shape[2]
        if part is None:
            return ref.at[j, owner]
        return ref.at[j, owner, pl.ds(part * (rows // 2), rows // 2)]

    items = [("w", 0), ("t", 0), ("t", 1), ("t", 2)] + [("w", j) for j in range(1, CHUNKS)]
    diag = me + to_x + to_y
    sends = [
        (me, None, dev_x), (me, None, dev_y), (me, None, dev_c),
        (dev_x, 0, dev_y), (dev_x, None, dev_c),
        (dev_y, 1, dev_x), (dev_y, None, dev_c),
        (diag, 0, dev_c), (diag, 1, dev_c),
    ]
    comes = [
        dev_x, dev_y, dev_c, diag, dev_x + to_c, diag, dev_y + to_c, diag + to_c, diag + to_c,
    ]

    def send(n, kind):
        owner, part, target = sends[kind]
        ref = piece(items[n], owner, part)
        return pltpu.make_async_remote_copy(
            ref, ref, send_sem.at[n, kind], recv_sem.at[n, kind],
            device_id=(section, target), device_id_type=MESH,
        )

    def arrive(n, kind):
        _, part, target = sends[kind]
        ref = piece(items[n], comes[kind], part)
        pltpu.make_async_remote_copy(
            ref, ref, send_sem.at[n, kind], recv_sem.at[n, kind],
            device_id=(section, target), device_id_type=MESH,
        ).wait_recv()

    def own(j):
        return latents.at[:, j * width : (j + 1) * width]

    def norm(source, slot):
        shift = mods[3 * slot : 3 * slot + 1, :]
        scale = 1.0 + mods[3 * slot + 1 : 3 * slot + 2, :]

        def rows16(i, _):
            rows = pl.ds(pl.multiple_of(i * 16, 16), 16)
            values = source[rows, :].astype(F32)
            centred = values - jnp.mean(values, axis=-1, keepdims=True)
            variance = jnp.mean(centred * centred, axis=-1, keepdims=True)
            gathered[slot, me, rows, :] = (
                centred * lax.rsqrt(variance + 1e-06) * scale + shift
            ).astype(BF16)
            return 0

        lax.fori_loop(0, tok // 16, rows16, 0)

    def take_over():
        @pl.when(has_prev)
        def _():
            hand_copy().wait_recv()

        @pl.when(section == 0)
        def _():
            raw[...] = jnp.zeros_like(raw)

        norm(raw, 2)

    def begin(n):
        kind, j = items[n]
        if kind == "w":
            load_out[j].wait()
        for kind_sent in (0, 1, 2):
            send(n, kind_sent).start()

    def forward(n):
        arrive(n, 0)
        send(n, 3).start()
        send(n, 4).start()
        arrive(n, 1)
        send(n, 5).start()
        send(n, 6).start()

    def last_forward(n):
        arrive(n, 3)
        send(n, 7).start()
        arrive(n, 5)
        send(n, 8).start()

    def finish(n):
        for kind in (2, 4, 6, 7, 8):
            arrive(n, kind)

    def mix_copy(slot, step, owner, target):
        return pltpu.make_async_remote_copy(
            mix_send.at[slot, target],
            mix_recv.at[slot, :, pl.ds(pl.multiple_of(owner * local, local), local)],
            mix_send_sem.at[slot, step], mix_recv_sem.at[slot, step],
            device_id=(section, target), device_id_type=MESH,
        )

    def project(slot):
        def step(i, _):
            hidden = gathered[slot, pl.ds(2 * i, 2)].reshape(2 * tok, width)
            rows = pl.ds(pl.multiple_of(i * 2 * tok, 2 * tok), 2 * tok)
            for part in range(3):
                qkv[rows, part * local : (part + 1) * local] = jnp.dot(
                    hidden, w_qkv[part], preferred_element_type=F32
                ).astype(BF16)
            return 0

        lax.fori_loop(0, peers // 2, step, 0)

    def queries(slot, first, end):
        def step(i, _):
            rows = pl.ds(pl.multiple_of(i * 2 * tok, 2 * tok), 2 * tok)
            for h in range(heads):
                a = h * HEAD_DIM
                query = qkv[rows, a : a + HEAD_DIM]
                keys = qkv[:, local + a : local + a + HEAD_DIM]
                vals = qkv[:, 2 * local + a : 2 * local + a + HEAD_DIM]
                scores = lax.dot_general(
                    query, keys, (((1,), (1,)), ((), ())), preferred_element_type=F32
                )
                top = jnp.max(scores, axis=-1, keepdims=True)
                probs = jnp.exp((scores - top) * HEAD_DIM ** (-0.5))
                total = jnp.sum(probs, axis=-1, keepdims=True)
                mixed = jnp.dot(probs.astype(BF16), vals, preferred_element_type=F32) / total
                mix_send[slot, pl.ds(2 * i, 2), :, a : a + HEAD_DIM] = mixed.astype(
                    BF16
                ).reshape(2, tok, HEAD_DIM)
            return 0

        lax.fori_loop(first, end, step, 0)

    def exchange(slot):
        mix_recv[slot, :, pl.ds(pl.multiple_of(me * local, local), local)] = mix_send[slot, me]
        for step in range(1, peers):
            mix_copy(slot, step, me, (me + step) % peers).start()

    def mix_arrive(slot):
        for step in range(1, peers):
            mix_copy(slot, step, (me + peers - step) % peers, (me + step) % peers).wait_recv()

    def project_out(j):
        table = w_out[j].reshape(peers * local, cols)
        at = slice(j * cols, (j + 1) * cols)
        for slot, source in ((2, raw), (0, own(0)), (1, own(1))):
            proj = jnp.dot(mix_recv[slot], table, preferred_element_type=F32)
            gate = mods[3 * slot + 2 : 3 * slot + 3, at]
            value = (source[:, at].astype(F32) + gate * proj).astype(BF16)
            if slot == 2:
                back[j] = value

                @pl.when(has_prev)
                def _():
                    back_copy(j).start()
            else:
                updated[:, slot * width + j * cols : slot * width + (j + 1) * cols] = value

    half = peers // 4
    w0, t0, t1, t2, w1, w2, w3 = range(len(items))
    norm(own(0), 0)
    begin(t0)
    begin(w0)
    norm(own(1), 1)
    forward(t0)
    begin(t1)
    forward(w0)
    take_over()
    last_forward(t0)
    finish(t0)
    load_qkv.wait()
    project(0)
    queries(0, 0, half)
    forward(t1)
    begin(t2)
    queries(0, half, 2 * half)
    exchange(0)
    last_forward(w0)
    last_forward(t1)
    finish(t1)
    project(1)
    queries(1, 0, half)
    forward(t2)
    begin(w1)
    queries(1, half, 2 * half)
    exchange(1)
    finish(w0)
    begin(w2)
    last_forward(t2)
    finish(t2)
    project(2)
    forward(w1)
    begin(w3)
    queries(2, 0, half)
    forward(w2)
    queries(2, half, 2 * half)
    exchange(2)
    last_forward(w1)
    forward(w3)
    last_forward(w2)
    for slot in range(3):
        mix_arrive(slot)
    project_out(0)
    finish(w1)
    project_out(1)
    finish(w2)
    project_out(2)
    last_forward(w3)
    finish(w3)
    project_out(3)

    for j in range(CHUNKS):
        @pl.when(has_next)
        def _():
            back_copy(j).wait_recv()

        for slot in range(slots):
            at = slice(slot * width + j * cols, slot * width + (j + 1) * cols)
            for i in range(tok // 16):
                rows = slice(i * 16, (i + 1) * 16)
                updated[rows, at] = jnp.where(
                    moves[slot][:, :cols], back_in[j, rows, :], updated[rows, at]
                )

        @pl.when(has_prev)
        def _():
            back_copy(j).wait_send()

    @pl.when(has_next)
    def _():
        hand_copy().wait_send()

    for n in range(len(items)):
        for kind in range(len(sends)):
            send(n, kind).wait_send()
    for slot in range(3):
        for step in range(1, peers):
            mix_copy(slot, step, me, (me + step) % peers).wait_send()


def kernel_body(sections, latents, timestep, target, qkv_weight, mod_weight, out_weight):
    tok, slots, width = latents.shape
    local = out_weight.shape[1]
    peers = width // local
    home = lax.axis_index("section")
    prev = jnp.maximum(home - 1, 0)
    own_steps = lax.dynamic_slice_in_dim(timestep, home * slots, slots)
    prev_steps = lax.dynamic_slice_in_dim(timestep, prev * slots, slots)
    prev_move = lax.dynamic_slice_in_dim(target, prev * slots, slots) == home
    came = jnp.sum(jnp.where(prev_move, prev_steps, 0), keepdims=True)
    mods = modulate(jnp.concatenate([own_steps, came]), mod_weight[0])
    mods = mods.reshape(3 * (slots + 1), width)
    vmem = pl.BlockSpec(memory_space=pltpu.VMEM)
    hbm = pl.BlockSpec(memory_space=pl.ANY)
    cols = width // CHUNKS
    n_items = slots + 1 + CHUNKS
    dma = pltpu.SemaphoreType.DMA
    updated = pl.pallas_call(
        functools.partial(block_kernel, sections),
        out_shape=jax.ShapeDtypeStruct((tok, slots * width), BF16),
        in_specs=[pl.BlockSpec(memory_space=pltpu.SMEM), vmem, vmem, hbm, hbm],
        out_specs=vmem,
        scratch_shapes=[
            pltpu.VMEM((tok, width), BF16),
            pltpu.VMEM((slots + 1, peers, tok, width), BF16),
            pltpu.VMEM((CHUNKS, peers, local, cols), BF16),
            pltpu.VMEM((3, width, local), BF16),
            pltpu.VMEM((peers * tok, 3 * local), BF16),
            pltpu.VMEM((slots + 1, peers, tok, local), BF16),
            pltpu.VMEM((slots + 1, tok, width), BF16),
            pltpu.VMEM((tok, width), BF16),
            pltpu.VMEM((CHUNKS, tok, cols), BF16),
            pltpu.VMEM((CHUNKS, tok, cols), BF16),
            dma((CHUNKS + 1,)),
            dma((n_items, 9)),
            dma((n_items, 9)),
            dma((slots + 1, peers)),
            dma((slots + 1, peers)),
            dma((2,)),
            dma((2, CHUNKS)),
        ],
        compiler_params=pltpu.CompilerParams(
            collective_id=0, has_side_effects=True, vmem_limit_bytes=60 * 1024 * 1024
        ),
    )(
        target,
        latents.reshape(tok, slots * width),
        mods,
        jnp.transpose(qkv_weight[0], (1, 0, 2)),
        out_weight[0],
    )
    return updated.reshape(tok, slots, width)


def solution(mesh):
    sections = mesh.shape["section"]
    plan = functools.partial(kernel_body, sections) if mesh.shape["tp"] == 8 else body

    return jax.shard_map(
        plan,
        mesh=mesh,
        in_specs=(
            P("tp", "section", None),
            P(),
            P(),
            P("section", None, None, "tp"),
            P("section", None, None, None),
            P("section", "tp", None),
        ),
        out_specs=P("tp", "section", None),
        check_vma=False,
    )
```

profile of v0, /device:TPU:0, one launch (start us, length us, event | category | flops | bytes accessed | tf_op | source)
XLA Modules:
  0.0 133.0 jit_solution(3525620636492677498)
XLA Ops:
  0.0 0.0 copy-start
  0.0 1.5 %fusion.9 = (s32[2]{0:T(128)S(1)}, s32[]{:T(128)}) fusion(s32[8]{0:T(128)} %param.7, s32[]{:T(128)S(6)} %select_n.11, s32[]{:T(128)S(6)} %select_n.12, s32[]{:T(128)S(6)} %axis_index.15, s32[8]{0:T(128)} %target.1), kind=kLoop, calls=%fused_computation.16 | loop fusion | flops 5 | bytes 48 | tf_op jit(solution)/shard_map/dynamic_slice | solution.py:445
  1.6 0.7 add_convert_fusion
  2.3 0.1 multiply_cosine_fusion
  2.4 0.0 copy-done
  2.4 1.3 fusion
  3.7 0.1 copy.7
  3.8 0.7 reshape.31.mods
  4.5 2.6 %copy.8 = bf16[16,8,2,2048]{3,1,2,0:T(8,128)(2,1)} copy(bf16[16,8,2,2048]{3,2,1,0:T(2,128)(2,1)} %bitcast.16) | data formatting | bytes 2097152
  7.1 123.3 %shard_map.64 = bf16[128,4096]{1,0:T(8,128)(2,1)} custom-call(s32[8]{0:T(128)} %target.1, bf16[128,4096]{1,0:T(8,128)(2,1)} %bitcast.13, f32[9,2048]{1,0:T(8,128)} %reshape.31.mods, bf16[3,2048,256]{2,1,0:T(8,128)(2,1)} %bitcast.14, bf16[256,2048]{1,0:T(8,128)(2,1)} %bitcast.15), custom_call_target="tpu_custom_call" | custom-call | tf_op jit(solution)/shard_map/pallas_call | solution.py:456
  130.4 2.6 %reshape.32 = bf16[128,2,2048]{2,1,0:T(2,128)(2,1)} reshape(bf16[128,4096]{1,0:T(8,128)(2,1)} %shard_map.64) | data formatting | bytes 2097152 | tf_op jit(solution)/shard_map/reshape | solution.py:490
  (1 shorter events, 0.0 us)
Async XLA Ops:
  0.0 2.4 %copy-start = (bf16[1,256,3,2048]{3,1,2,0:T(8,128)(2,1)S(1)}, bf16[1,256,3,2048]{3,1,2,0:T(8,128)(2,1)}, u32[]{:S(2)}) copy-start(bf16[1,256,3,2048]{3,1,2,0:T(8,128)(2,1)} %param.10) | copy-start | bytes 9437188
where the time goes:
time: 133 us
  Pallas kernels  123 us (92%)
  local copies, waits for them, and re-layouts  5.94 us (4%)
  other arithmetic  2.39 us (2%)
  matrix products  1.33 us (1%)
    pallas_call x1, Pallas kernels, kernel_body(): pl.pallas_call(functools.partial(block_kernel, sections), out_shape=jax.S...  123 us

commit v1 on v0

--- a/solution.py
+++ b/solution.py
@@ -119,10 +119,12 @@
 def block_kernel(
     sections, target, latents, mods, w_qkv_hbm, w_out_hbm,
     updated,
-    outgoing, gathered, w_out, w_qkv, qkv, mix_send, mix_recv, raw, back, back_in,
-    load_sem, send_sem, recv_sem, mix_send_sem, mix_recv_sem, hand_sem, back_sem,
+    gathered, w_out, w_qkv, qkv, mix_send, mix_recv, mods_in, back, back_in,
+    load_sem, send_sem, recv_sem, mix_send_sem, mix_recv_sem, hand_sem, share_sem, mods_sem,
+    back_sem,
 ):
-    tok, width = raw.shape
+    tok = latents.shape[0]
+    width = w_qkv.shape[1]
     slots = latents.shape[1] // width
     local = w_out.shape[2]
     heads = local // HEAD_DIM
@@ -137,6 +139,7 @@
     to_y = 4 - 8 * y
     to_c = 1 - 2 * core
     dev_x, dev_y, dev_c = me + to_x, me + to_y, me + to_c
+    diag = me + to_x + to_y
     has_prev = section > 0
     has_next = section < sections - 1
 
@@ -168,10 +171,10 @@
     beside = jnp.minimum(section, 1) + jnp.minimum(sections - 1 - section, 1)
     pl.semaphore_wait(barrier, peers - 1 + beside)
 
-    def hand_copy():
+    def mods_copy():
         return pltpu.make_async_remote_copy(
-            outgoing, raw, hand_sem.at[0], hand_sem.at[1],
-            device_id=(section + 1, me), device_id_type=MESH,
+            mods.at[2], mods_in.at[0], mods_sem.at[0], mods_sem.at[1],
+            device_id=(section - 1, me), device_id_type=MESH,
         )
 
     def back_copy(j):
@@ -180,21 +183,15 @@
             device_id=(section - 1, me), device_id_type=MESH,
         )
 
-    moves = [
-        jnp.broadcast_to((target[section * slots + j] != section).astype(jnp.int32), (16, width)) != 0
-        for j in range(slots)
-    ]
-
-    def choose(i, _):
-        rows = pl.ds(pl.multiple_of(i * 16, 16), 16)
-        outgoing[rows, :] = jnp.where(moves[0], latents[rows, :width], latents[rows, width:])
-        return 0
-
-    lax.fori_loop(0, tok // 16, choose, 0)
-
-    @pl.when(has_next)
+    @pl.when(has_prev)
     def _():
-        hand_copy().start()
+        mods_copy().start()
+
+    flags = [(target[section * slots + j] != section).astype(jnp.int32) for j in range(slots)]
+    any_move = jnp.maximum(flags[0], flags[1])
+
+    def mask(flag, shape):
+        return jnp.broadcast_to(flag, shape) != 0
 
     def piece(item, owner, part):
         kind, j = item
@@ -204,8 +201,7 @@
             return ref.at[j, owner]
         return ref.at[j, owner, pl.ds(part * (rows // 2), rows // 2)]
 
-    items = [("w", 0), ("t", 0), ("t", 1), ("t", 2)] + [("w", j) for j in range(1, CHUNKS)]
-    diag = me + to_x + to_y
+    items = [("w", 0), ("t", 0), ("t", 1)] + [("w", j) for j in range(1, CHUNKS)]
     sends = [
         (me, None, dev_x), (me, None, dev_y), (me, None, dev_c),
         (dev_x, 0, dev_y), (dev_x, None, dev_c),
@@ -232,16 +228,60 @@
             device_id=(section, target), device_id_type=MESH,
         ).wait_recv()
 
-    def own(j):
-        return latents.at[:, j * width : (j + 1) * width]
-
-    def norm(source, slot):
-        shift = mods[3 * slot : 3 * slot + 1, :]
-        scale = 1.0 + mods[3 * slot + 1 : 3 * slot + 2, :]
+    handed = [(me, None), (dev_x, None), (dev_y, None), (diag, 0), (diag, 1)]
+
+    def hand_copy(k):
+        owner, part = handed[k]
+        return pltpu.make_async_remote_copy(
+            piece(("t", 0), owner, part), piece(("t", 2), owner, part),
+            hand_sem.at[0, k], hand_sem.at[1, k],
+            device_id=(section + 1, me), device_id_type=MESH,
+        )
+
+    def hand(k):
+        @pl.when(has_next)
+        def _():
+            hand_copy(k).start()
+
+    def share_copy(k, shift):
+        owner, part = handed[k]
+        ref = piece(("t", 2), owner + shift, part)
+        return pltpu.make_async_remote_copy(
+            ref, ref, share_sem.at[0, k], share_sem.at[1, k],
+            device_id=(section, dev_c), device_id_type=MESH,
+        )
+
+    def share(*ks):
+        @pl.when(has_prev)
+        def _():
+            for k in ks:
+                hand_copy(k).wait_recv()
+                share_copy(k, 0).start()
+
+    def shared(*ks):
+        @pl.when(has_prev)
+        def _():
+            for k in ks:
+                share_copy(k, to_c).wait_recv()
+
+    def own(slot, rows, at):
+        first = latents[rows, at]
+        second = latents[rows, slice(width + at.start, width + at.stop)]
+        pick = mask(flags[0], first.shape)
+        return jnp.where(pick, first, second) if slot == 0 else jnp.where(pick, second, first)
+
+    def norm(slot):
+        shift = mods[slot, 0:1, :]
+        scale = mods[slot, 1:2, :]
+        if slot == 0:
+            moved = mask(any_move, shift.shape)
+            shift = jnp.where(moved, mods_in[0, 0:1, :], shift)
+            scale = jnp.where(moved, mods_in[0, 1:2, :], scale)
+        scale = 1.0 + scale
 
         def rows16(i, _):
             rows = pl.ds(pl.multiple_of(i * 16, 16), 16)
-            values = source[rows, :].astype(F32)
+            values = own(slot, rows, slice(0, width)).astype(F32)
             centred = values - jnp.mean(values, axis=-1, keepdims=True)
             variance = jnp.mean(centred * centred, axis=-1, keepdims=True)
             gathered[slot, me, rows, :] = (
@@ -251,17 +291,6 @@
 
         lax.fori_loop(0, tok // 16, rows16, 0)
 
-    def take_over():
-        @pl.when(has_prev)
-        def _():
-            hand_copy().wait_recv()
-
-        @pl.when(section == 0)
-        def _():
-            raw[...] = jnp.zeros_like(raw)
-
-        norm(raw, 2)
-
     def begin(n):
         kind, j = items[n]
         if kind == "w":
@@ -273,19 +302,23 @@
         arrive(n, 0)
         send(n, 3).start()
         send(n, 4).start()
+        if n == t0:
+            hand(1)
         arrive(n, 1)
         send(n, 5).start()
         send(n, 6).start()
+        if n == t0:
+            hand(2)
 
     def last_forward(n):
         arrive(n, 3)
         send(n, 7).start()
+        if n == t0:
+            hand(3)
         arrive(n, 5)
         send(n, 8).start()
-
-    def finish(n):
-        for kind in (2, 4, 6, 7, 8):
-            arrive(n, kind)
+        if n == t0:
+            hand(4)
 
     def mix_copy(slot, step, owner, target):
         return pltpu.make_async_remote_copy(
@@ -295,26 +328,27 @@
             device_id=(section, target), device_id_type=MESH,
         )
 
-    def project(slot):
-        def step(i, _):
-            hidden = gathered[slot, pl.ds(2 * i, 2)].reshape(2 * tok, width)
-            rows = pl.ds(pl.multiple_of(i * 2 * tok, 2 * tok), 2 * tok)
+    def project(slot, first, end):
+        def step(k, _):
+            chip = (y + k // 2) % 2 * 2 + (x + k % 2) % 2
+            hidden = gathered[slot, pl.ds(2 * chip, 2)].reshape(2 * tok, width)
+            rows = pl.ds(pl.multiple_of(chip * 2 * tok, 2 * tok), 2 * tok)
             for part in range(3):
-                qkv[rows, part * local : (part + 1) * local] = jnp.dot(
+                qkv[slot, rows, part * local : (part + 1) * local] = jnp.dot(
                     hidden, w_qkv[part], preferred_element_type=F32
                 ).astype(BF16)
             return 0
 
-        lax.fori_loop(0, peers // 2, step, 0)
+        lax.fori_loop(first, end, step, 0)
 
     def queries(slot, first, end):
         def step(i, _):
             rows = pl.ds(pl.multiple_of(i * 2 * tok, 2 * tok), 2 * tok)
             for h in range(heads):
                 a = h * HEAD_DIM
-                query = qkv[rows, a : a + HEAD_DIM]
-                keys = qkv[:, local + a : local + a + HEAD_DIM]
-                vals = qkv[:, 2 * local + a : 2 * local + a + HEAD_DIM]
+                query = qkv[slot, rows, a : a + HEAD_DIM]
+                keys = qkv[slot, :, local + a : local + a + HEAD_DIM]
+                vals = qkv[slot, :, 2 * local + a : 2 * local + a + HEAD_DIM]
                 scores = lax.dot_general(
                     query, keys, (((1,), (1,)), ((), ())), preferred_element_type=F32
                 )
@@ -341,71 +375,89 @@
     def project_out(j):
         table = w_out[j].reshape(peers * local, cols)
         at = slice(j * cols, (j + 1) * cols)
-        for slot, source in ((2, raw), (0, own(0)), (1, own(1))):
+        proj = jnp.dot(mix_recv[2], table, preferred_element_type=F32)
+        back[j] = (mods[2, 2:3, at] * proj).astype(BF16)
+
+        @pl.when(has_prev)
+        def _():
+            back_copy(j).start()
+
+        values = []
+        for slot in range(slots):
             proj = jnp.dot(mix_recv[slot], table, preferred_element_type=F32)
-            gate = mods[3 * slot + 2 : 3 * slot + 3, at]
-            value = (source[:, at].astype(F32) + gate * proj).astype(BF16)
-            if slot == 2:
-                back[j] = value
-
-                @pl.when(has_prev)
-                def _():
-                    back_copy(j).start()
-            else:
-                updated[:, slot * width + j * cols : slot * width + (j + 1) * cols] = value
+            raw = own(slot, slice(None), at).astype(F32)
+            values.append((raw + mods[slot, 2:3, at] * proj).astype(BF16))
+        pick = mask(flags[0], values[0].shape)
+        updated[:, at] = jnp.where(pick, values[0], values[1])
+        updated[:, slice(width + at.start, width + at.stop)] = jnp.where(
+            pick, values[1], values[0]
+        )
 
     half = peers // 4
-    w0, t0, t1, t2, w1, w2, w3 = range(len(items))
-    norm(own(0), 0)
+    w0, t0, t1, w1, w2, w3 = range(len(items))
+    begin(w0)
+
+    @pl.when(has_next)
+    def _():
+        mods_copy().wait_recv()
+
+    norm(0)
     begin(t0)
-    begin(w0)
-    norm(own(1), 1)
-    forward(t0)
+    hand(0)
+    norm(1)
     begin(t1)
     forward(w0)
-    take_over()
+    load_qkv.wait()
+    forward(t0)
+    share(0)
+    for kind in (2, 4, 6):
+        arrive(t0, kind)
+    project(0, 0, 3)
+    last_forward(w0)
+    forward(t1)
+    begin(w1)
+    for kind in (2, 4, 6):
+        arrive(t1, kind)
+    project(1, 0, 3)
     last_forward(t0)
-    finish(t0)
-    load_qkv.wait()
-    project(0)
+    for kind in (7, 8):
+        arrive(t0, kind)
+    project(0, 3, 4)
+    share(1)
     queries(0, 0, half)
-    forward(t1)
-    begin(t2)
+    begin(w2)
+    last_forward(t1)
     queries(0, half, 2 * half)
     exchange(0)
-    last_forward(w0)
-    last_forward(t1)
-    finish(t1)
-    project(1)
+    for kind in (7, 8):
+        arrive(t1, kind)
+    share(2)
+    project(1, 3, 4)
+    forward(w1)
     queries(1, 0, half)
-    forward(t2)
-    begin(w1)
+    begin(w3)
+    forward(w2)
+    share(3, 4)
     queries(1, half, 2 * half)
     exchange(1)
-    finish(w0)
-    begin(w2)
-    last_forward(t2)
-    finish(t2)
-    project(2)
-    forward(w1)
-    begin(w3)
+    last_forward(w1)
+    shared(0, 1, 2, 3, 4)
+    project(2, 0, 4)
+    forward(w3)
     queries(2, 0, half)
-    forward(w2)
+    last_forward(w2)
     queries(2, half, 2 * half)
     exchange(2)
-    last_forward(w1)
-    forward(w3)
-    last_forward(w2)
+    last_forward(w3)
+    for kind in (2, 4, 6, 7, 8):
+        arrive(w0, kind)
     for slot in range(3):
         mix_arrive(slot)
     project_out(0)
-    finish(w1)
-    project_out(1)
-    finish(w2)
-    project_out(2)
-    last_forward(w3)
-    finish(w3)
-    project_out(3)
+    for n, j in ((w1, 1), (w2, 2), (w3, 3)):
+        for kind in (2, 4, 6, 7, 8):
+            arrive(n, kind)
+        project_out(j)
 
     for j in range(CHUNKS):
         @pl.when(has_next)
@@ -416,8 +468,9 @@
             at = slice(slot * width + j * cols, slot * width + (j + 1) * cols)
             for i in range(tok // 16):
                 rows = slice(i * 16, (i + 1) * 16)
+                returned = latents[rows, at].astype(F32) + back_in[j, rows, :].astype(F32)
                 updated[rows, at] = jnp.where(
-                    moves[slot][:, :cols], back_in[j, rows, :], updated[rows, at]
+                    mask(flags[slot], (16, cols)), returned.astype(BF16), updated[rows, at]
                 )
 
         @pl.when(has_prev)
@@ -426,7 +479,14 @@
 
     @pl.when(has_next)
     def _():
-        hand_copy().wait_send()
+        for k in range(len(handed)):
+            hand_copy(k).wait_send()
+
+    @pl.when(has_prev)
+    def _():
+        mods_copy().wait_send()
+        for k in range(len(handed)):
+            share_copy(k, 0).wait_send()
 
     for n in range(len(items)):
         for kind in range(len(sends)):
@@ -446,12 +506,13 @@
     prev_steps = lax.dynamic_slice_in_dim(timestep, prev * slots, slots)
     prev_move = lax.dynamic_slice_in_dim(target, prev * slots, slots) == home
     came = jnp.sum(jnp.where(prev_move, prev_steps, 0), keepdims=True)
-    mods = modulate(jnp.concatenate([own_steps, came]), mod_weight[0])
-    mods = mods.reshape(3 * (slots + 1), width)
+    first = lax.dynamic_slice_in_dim(target, home * slots, 1) != home
+    turned = jnp.where(first, own_steps, own_steps[::-1])
+    mods = modulate(jnp.concatenate([turned, came]), mod_weight[0])
     vmem = pl.BlockSpec(memory_space=pltpu.VMEM)
     hbm = pl.BlockSpec(memory_space=pl.ANY)
     cols = width // CHUNKS
-    n_items = slots + 1 + CHUNKS
+    n_items = slots + CHUNKS
     dma = pltpu.SemaphoreType.DMA
     updated = pl.pallas_call(
         functools.partial(block_kernel, sections),
@@ -459,14 +520,13 @@
         in_specs=[pl.BlockSpec(memory_space=pltpu.SMEM), vmem, vmem, hbm, hbm],
         out_specs=vmem,
         scratch_shapes=[
-            pltpu.VMEM((tok, width), BF16),
             pltpu.VMEM((slots + 1, peers, tok, width), BF16),
             pltpu.VMEM((CHUNKS, peers, local, cols), BF16),
             pltpu.VMEM((3, width, local), BF16),
-            pltpu.VMEM((peers * tok, 3 * local), BF16),
+            pltpu.VMEM((slots + 1, peers * tok, 3 * local), BF16),
             pltpu.VMEM((slots + 1, peers, tok, local), BF16),
             pltpu.VMEM((slots + 1, tok, width), BF16),
-            pltpu.VMEM((tok, width), BF16),
+            pltpu.VMEM((1, 3, width), F32),
             pltpu.VMEM((CHUNKS, tok, cols), BF16),
             pltpu.VMEM((CHUNKS, tok, cols), BF16),
             dma((CHUNKS + 1,)),
@@ -474,6 +534,8 @@
             dma((n_items, 9)),
             dma((slots + 1, peers)),
             dma((slots + 1, peers)),
+            dma((2, 5)),
+            dma((2, 5)),
             dma((2,)),
             dma((2, CHUNKS)),
         ],

time: 133 us -> 119 us (0.89)
  Pallas kernels: 123 us -> 108 us
    pallas_call x1, Pallas kernels: 123 us -> 108 us  [kernel_body(): pl.pallas_call(functools.partial(block_kernel, sections), out_shape=jax.S...]
    dynamic_slice x0 -> x1, local copies, waits for them, and re-layouts: none -> 1.45 us  [kernel_body(): first = lax.dynamic_slice_in_dim(target, home * slots, 1) != home]
where the time goes in v1:
time: 119 us
  Pallas kernels  108 us (91%)
  local copies, waits for them, and re-layouts  6.21 us (5%)
  other arithmetic  2.43 us (2%)
  matrix products  1.33 us (1%)
    pallas_call x1, Pallas kernels, kernel_body(): pl.pallas_call(functools.partial(block_kernel, sections), out_shape=jax.S...  108 us
    reshape x1, local copies, waits for them, and re-layouts, kernel_body(): return updated.reshape(tok, slots, width)  2.62 us

profile of v1, /device:TPU:0, one launch (start us, length us, event | category | flops | bytes accessed | tf_op | source)
XLA Modules:
  0.0 118.6 jit_solution(3051759549521481122)
XLA Ops:
  0.0 0.0 copy-start
  0.0 1.5 %dynamic_slice.12 = s32[1]{0:T(128)} dynamic-slice(s32[8]{0:T(128)} %target.1, s32[]{:T(128)S(6)} %select_n.16), dynamic_slice_sizes={1} | dynamic-slice | bytes 12 | tf_op jit(solution)/shard_map/dynamic_slice | solution.py:509
  2.1 1.5 %fusion.9 = (s32[2]{0:T(128)S(1)}, s32[]{:T(128)}) fusion(s32[8]{0:T(128)} %param.7, s32[]{:T(128)S(6)} %select_n.16, s32[]{:T(128)S(6)} %select_n.18, s32[]{:T(128)} %axis_index.15, s32[8]{0:T(128)} %target.1), kind=kLoop, calls=%fused_computation.17 | loop fusion | flops 5 | bytes 48 | tf_op jit(solution)/shard_map/dynamic_slice | solution.py:505
  3.6 0.1 rev.3
  3.7 0.0 copy-start.1
  3.7 0.8 add_convert_fusion
  4.5 0.1 multiply_cosine_fusion
  4.6 0.0 copy-done
  4.6 1.3 %fusion = f32[3,3,2048]{2,0,1:T(4,128)S(1)} fusion(bf16[1,256,3,2048]{3,1,2,0:T(8,128)(2,1)S(1)} %copy-done, f32[3,128]{1,0:T(4,128)S(1)} %get-tuple-element.6, f32[3,128]{1,0:T(4,128)S(1)} %get-tuple-element.5), kind=kOutput, calls=%fused_computation | convolution fusion | flops 56626944 | bytes 3222528 | tf_op jit(solution)/shard_map/bf,fcd->bcd/dot_general | solution.py:31
  6.0 0.7 copy.7.mods
  6.7 0.0 copy-done.1
  6.7 1.3 %copy.8 = bf16[16,8,2,2048]{3,1,2,0:T(8,128)(2,1)} copy(bf16[16,8,2,2048]{3,2,1,0:T(2,128)(2,1)S(1)} %bitcast.18) | data formatting | bytes 2097152
  8.0 108.0 %shard_map.64 = bf16[128,4096]{1,0:T(8,128)(2,1)} custom-call(s32[8]{0:T(128)} %target.1, bf16[128,4096]{1,0:T(8,128)(2,1)} %bitcast.15, f32[3,3,2048]{2,1,0:T(4,128)} %copy.7.mods, bf16[3,2048,256]{2,1,0:T(8,128)(2,1)} %bitcast.16, bf16[256,2048]{1,0:T(8,128)(2,1)} %bitcast.17), custom_call_target="tpu_custom_call" | custom-call | tf_op jit(solution)/shard_map/pallas_call | solution.py:517
  116.0 2.6 %reshape.28 = bf16[128,2,2048]{2,1,0:T(2,128)(2,1)} reshape(bf16[128,4096]{1,0:T(8,128)(2,1)} %shard_map.64) | data formatting | bytes 2097152 | tf_op jit(solution)/shard_map/reshape | solution.py:552
  (2 shorter events, 0.0 us)
Async XLA Ops:
  0.0 4.6 %copy-start = (bf16[1,256,3,2048]{3,1,2,0:T(8,128)(2,1)S(1)}, bf16[1,256,3,2048]{3,1,2,0:T(8,128)(2,1)}, u32[]{:S(2)}) copy-start(bf16[1,256,3,2048]{3,1,2,0:T(8,128)(2,1)} %param.10) | copy-start | bytes 9437188
  3.7 3.0 %copy-start.1 = (bf16[128,2,2048]{2,1,0:T(2,128)(2,1)S(1)}, bf16[128,2,2048]{2,1,0:T(2,128)(2,1)}, u32[]{:S(2)}) copy-start(bf16[128,2,2048]{2,1,0:T(2,128)(2,1)} %param.6) | copy-start | bytes 3145732

commit v2 on v1

--- a/solution.py
+++ b/solution.py
@@ -117,15 +117,14 @@
 
 
 def block_kernel(
-    sections, target, latents, mods, w_qkv_hbm, w_out_hbm,
-    updated,
-    gathered, w_out, w_qkv, qkv, mix_send, mix_recv, mods_in, back, back_in,
+    sections, target, timestep, latents_hbm, w_mod_hbm, w_qkv_hbm, w_out_hbm,
+    updated_hbm,
+    latents, raw, w_mod, mods, mods_out, mods_in, gathered, w_out, w_qkv, qkv, mix_send, mix_recv,
+    back, back_in, hold, updated,
     load_sem, send_sem, recv_sem, mix_send_sem, mix_recv_sem, hand_sem, share_sem, mods_sem,
-    back_sem,
+    back_sem, store_sem,
 ):
-    tok = latents.shape[0]
-    width = w_qkv.shape[1]
-    slots = latents.shape[1] // width
+    tok, slots, width = latents.shape
     local = w_out.shape[2]
     heads = local // HEAD_DIM
     peers = gathered.shape[1]
@@ -143,16 +142,17 @@
     has_prev = section > 0
     has_next = section < sections - 1
 
-    load_qkv = pltpu.make_async_copy(w_qkv_hbm, w_qkv, load_sem.at[CHUNKS])
     load_out = [
         pltpu.make_async_copy(
             w_out_hbm.at[:, j * cols : (j + 1) * cols], w_out.at[j, me], load_sem.at[j]
         )
         for j in range(CHUNKS)
     ]
-    for copy in load_out:
+    load_qkv = pltpu.make_async_copy(w_qkv_hbm, w_qkv, load_sem.at[CHUNKS])
+    load_mod = pltpu.make_async_copy(w_mod_hbm, w_mod, load_sem.at[CHUNKS + 1])
+    load_latents = pltpu.make_async_copy(latents_hbm, latents, load_sem.at[CHUNKS + 2])
+    for copy in (load_out[0], load_mod, load_latents, *load_out[1:], load_qkv):
         copy.start()
-    load_qkv.start()
 
     barrier = pltpu.get_barrier_semaphore()
     for step in range(1, peers):
@@ -173,7 +173,7 @@
 
     def mods_copy():
         return pltpu.make_async_remote_copy(
-            mods.at[2], mods_in.at[0], mods_sem.at[0], mods_sem.at[1],
+            mods_out, mods_in, mods_sem.at[0], mods_sem.at[1],
             device_id=(section - 1, me), device_id_type=MESH,
         )
 
@@ -182,10 +182,6 @@
             back.at[j], back_in.at[j], back_sem.at[0, j], back_sem.at[1, j],
             device_id=(section - 1, me), device_id_type=MESH,
         )
-
-    @pl.when(has_prev)
-    def _():
-        mods_copy().start()
 
     flags = [(target[section * slots + j] != section).astype(jnp.int32) for j in range(slots)]
     any_move = jnp.maximum(flags[0], flags[1])
@@ -264,24 +260,66 @@
             for k in ks:
                 share_copy(k, to_c).wait_recv()
 
-    def own(slot, rows, at):
-        first = latents[rows, at]
-        second = latents[rows, slice(width + at.start, width + at.stop)]
-        pick = mask(flags[0], first.shape)
-        return jnp.where(pick, first, second) if slot == 0 else jnp.where(pick, second, first)
+    def modulation():
+        prev = jnp.maximum(section - 1, 0)
+        came = sum(
+            jnp.where(target[prev * slots + j] == section, timestep[prev * slots + j], 0)
+            for j in range(slots)
+        )
+        step0, step1 = timestep[section * slots], timestep[section * slots + 1]
+        step_a = jnp.where(flags[0] != 0, step0, step1)
+        step_b = jnp.where(flags[0] != 0, step1, step0)
+        half_width = FREQ // 2
+        row = lax.broadcasted_iota(jnp.int32, (8, half_width), 0)
+        steps = jnp.where(row == 0, step_a, jnp.where(row == 1, step_b, came)).astype(F32)
+        lane = lax.broadcasted_iota(jnp.int32, (8, half_width), 1).astype(F32)
+        angles = steps * jnp.exp(-math.log(10000.0) * lane / half_width)
+        embed = jnp.concatenate([jnp.cos(angles), jnp.sin(angles)], axis=1)
+        rest = embed / (1.0 + jnp.exp(-embed))
+        terms = []
+        for _ in range(3):
+            terms.append(rest.astype(BF16).astype(F32))
+            rest = rest - terms[-1]
+        terms = jnp.concatenate(terms, axis=0).astype(BF16)
+        load_mod.wait()
+        for part in range(3):
+            sums = jnp.dot(terms, w_mod[part], preferred_element_type=F32)
+            mods[part] = sums[0:8] + sums[8:16] + sums[16:24]
+        quarter = width // 4
+        for part in range(2):
+            for q in range(4):
+                mods_out[part * 4 + q : part * 4 + q + 1, :] = mods[
+                    part, 2:3, q * quarter : (q + 1) * quarter
+                ]
+
+        @pl.when(has_prev)
+        def _():
+            mods_copy().start()
+
+    def unpack():
+        for i in range(tok // 16):
+            rows = slice(i * 16, (i + 1) * 16)
+            both = pltpu.einshape("asc->sac", latents[rows])
+            pick = mask(flags[0], (16, width))
+            raw[0, rows, :] = jnp.where(pick, both[0], both[1])
+            raw[1, rows, :] = jnp.where(pick, both[1], both[0])
 
     def norm(slot):
-        shift = mods[slot, 0:1, :]
-        scale = mods[slot, 1:2, :]
+        shift = mods[0, slot : slot + 1, :]
+        scale = mods[1, slot : slot + 1, :]
         if slot == 0:
             moved = mask(any_move, shift.shape)
-            shift = jnp.where(moved, mods_in[0, 0:1, :], shift)
-            scale = jnp.where(moved, mods_in[0, 1:2, :], scale)
+            came = [
+                jnp.concatenate([mods_in[4 * part + q : 4 * part + q + 1, :] for q in range(4)], axis=1)
+                for part in range(2)
+            ]
+            shift = jnp.where(moved, came[0], shift)
+            scale = jnp.where(moved, came[1], scale)
         scale = 1.0 + scale
 
         def rows16(i, _):
             rows = pl.ds(pl.multiple_of(i * 16, 16), 16)
-            values = own(slot, rows, slice(0, width)).astype(F32)
+            values = raw[slot, rows, :].astype(F32)
             centred = values - jnp.mean(values, axis=-1, keepdims=True)
             variance = jnp.mean(centred * centred, axis=-1, keepdims=True)
             gathered[slot, me, rows, :] = (
@@ -372,30 +410,51 @@
         for step in range(1, peers):
             mix_copy(slot, step, (me + peers - step) % peers, (me + step) % peers).wait_recv()
 
-    def project_out(j):
+    def project_out(slot, j):
         table = w_out[j].reshape(peers * local, cols)
         at = slice(j * cols, (j + 1) * cols)
-        proj = jnp.dot(mix_recv[2], table, preferred_element_type=F32)
-        back[j] = (mods[2, 2:3, at] * proj).astype(BF16)
-
-        @pl.when(has_prev)
+        change = mods[2, slot : slot + 1, at] * jnp.dot(
+            mix_recv[slot], table, preferred_element_type=F32
+        )
+        if slot == 2:
+            back[j] = change.astype(BF16)
+
+            @pl.when(has_prev)
+            def _():
+                back_copy(j).start()
+
+            return
+        hold[slot, j] = (raw[slot, :, at].astype(F32) + change).astype(BF16)
+
+    def store_copy(j):
+        at = slice(j * cols, (j + 1) * cols)
+        return pltpu.make_async_copy(
+            updated.at[:, :, at], updated_hbm.at[:, :, at], store_sem.at[j]
+        )
+
+    def write(j):
+        @pl.when(has_next)
         def _():
-            back_copy(j).start()
-
-        values = []
-        for slot in range(slots):
-            proj = jnp.dot(mix_recv[slot], table, preferred_element_type=F32)
-            raw = own(slot, slice(None), at).astype(F32)
-            values.append((raw + mods[slot, 2:3, at] * proj).astype(BF16))
-        pick = mask(flags[0], values[0].shape)
-        updated[:, at] = jnp.where(pick, values[0], values[1])
-        updated[:, slice(width + at.start, width + at.stop)] = jnp.where(
-            pick, values[1], values[0]
-        )
+            back_copy(j).wait_recv()
+
+        at = slice(j * cols, (j + 1) * cols)
+        pick = mask(flags[0], (16, cols))
+        moved = mask(any_move, (16, cols))
+        for i in range(tok // 16):
+            rows = slice(i * 16, (i + 1) * 16)
+            returned = raw[0, rows, at].astype(F32) + back_in[j, rows, :].astype(F32)
+            first = jnp.where(moved, returned.astype(BF16), hold[0, j, rows, :])
+            second = hold[1, j, rows, :]
+            updated[rows, 0, at] = jnp.where(pick, first, second)
+            updated[rows, 1, at] = jnp.where(pick, second, first)
+        store_copy(j).start()
 
     half = peers // 4
     w0, t0, t1, w1, w2, w3 = range(len(items))
     begin(w0)
+    modulation()
+    load_latents.wait()
+    unpack()
 
     @pl.when(has_next)
     def _():
@@ -404,74 +463,73 @@
     norm(0)
     begin(t0)
     hand(0)
+    begin(w1)
     norm(1)
-    begin(t1)
     forward(w0)
     load_qkv.wait()
+    arrive(t0, 2)
+    project(0, 0, 1)
     forward(t0)
+    begin(t1)
+    for kind in (4, 6):
+        arrive(t0, kind)
+    project(0, 1, 3)
     share(0)
-    for kind in (2, 4, 6):
-        arrive(t0, kind)
-    project(0, 0, 3)
     last_forward(w0)
-    forward(t1)
-    begin(w1)
-    for kind in (2, 4, 6):
-        arrive(t1, kind)
-    project(1, 0, 3)
+    forward(w1)
     last_forward(t0)
     for kind in (7, 8):
         arrive(t0, kind)
     project(0, 3, 4)
-    share(1)
+    begin(w2)
     queries(0, 0, half)
-    begin(w2)
-    last_forward(t1)
+    last_forward(w1)
     queries(0, half, 2 * half)
     exchange(0)
+    share(1)
+    shared(0, 1)
+    project(2, 0, 2)
+    forward(t1)
+    begin(w3)
+    for kind in (2, 4, 6):
+        arrive(t1, kind)
+    project(1, 0, 3)
+    share(2)
+    forward(w2)
+    last_forward(t1)
+    share(3, 4)
+    shared(2, 3, 4)
+    project(2, 2, 4)
+    queries(2, 0, half)
+    last_forward(w2)
+    forward(w3)
+    queries(2, half, 2 * half)
+    exchange(2)
     for kind in (7, 8):
         arrive(t1, kind)
-    share(2)
     project(1, 3, 4)
-    forward(w1)
+    last_forward(w3)
     queries(1, 0, half)
-    begin(w3)
-    forward(w2)
-    share(3, 4)
+    mix_arrive(2)
+    for n, j in ((w0, 0), (w1, 1)):
+        for kind in (2, 4, 6, 7, 8):
+            arrive(n, kind)
+        project_out(2, j)
     queries(1, half, 2 * half)
     exchange(1)
-    last_forward(w1)
-    shared(0, 1, 2, 3, 4)
-    project(2, 0, 4)
-    forward(w3)
-    queries(2, 0, half)
-    last_forward(w2)
-    queries(2, half, 2 * half)
-    exchange(2)
-    last_forward(w3)
-    for kind in (2, 4, 6, 7, 8):
-        arrive(w0, kind)
-    for slot in range(3):
-        mix_arrive(slot)
-    project_out(0)
-    for n, j in ((w1, 1), (w2, 2), (w3, 3)):
+    for n, j in ((w2, 2), (w3, 3)):
         for kind in (2, 4, 6, 7, 8):
             arrive(n, kind)
-        project_out(j)
-
+        project_out(2, j)
+    mix_arrive(0)
     for j in range(CHUNKS):
-        @pl.when(has_next)
-        def _():
-            back_copy(j).wait_recv()
-
-        for slot in range(slots):
-            at = slice(slot * width + j * cols, slot * width + (j + 1) * cols)
-            for i in range(tok // 16):
-                rows = slice(i * 16, (i + 1) * 16)
-                returned = latents[rows, at].astype(F32) + back_in[j, rows, :].astype(F32)
-                updated[rows, at] = jnp.where(
-                    mask(flags[slot], (16, cols)), returned.astype(BF16), updated[rows, at]
-                )
+        project_out(0, j)
+    mix_arrive(1)
+    for j in range(CHUNKS):
+        project_out(1, j)
+        write(j)
+    for j in range(CHUNKS):
+        store_copy(j).wait()
 
         @pl.when(has_prev)
         def _():
@@ -500,36 +558,34 @@
     tok, slots, width = latents.shape
     local = out_weight.shape[1]
     peers = width // local
-    home = lax.axis_index("section")
-    prev = jnp.maximum(home - 1, 0)
-    own_steps = lax.dynamic_slice_in_dim(timestep, home * slots, slots)
-    prev_steps = lax.dynamic_slice_in_dim(timestep, prev * slots, slots)
-    prev_move = lax.dynamic_slice_in_dim(target, prev * slots, slots) == home
-    came = jnp.sum(jnp.where(prev_move, prev_steps, 0), keepdims=True)
-    first = lax.dynamic_slice_in_dim(target, home * slots, 1) != home
-    turned = jnp.where(first, own_steps, own_steps[::-1])
-    mods = modulate(jnp.concatenate([turned, came]), mod_weight[0])
-    vmem = pl.BlockSpec(memory_space=pltpu.VMEM)
+    smem = pl.BlockSpec(memory_space=pltpu.SMEM)
     hbm = pl.BlockSpec(memory_space=pl.ANY)
     cols = width // CHUNKS
     n_items = slots + CHUNKS
     dma = pltpu.SemaphoreType.DMA
     updated = pl.pallas_call(
         functools.partial(block_kernel, sections),
-        out_shape=jax.ShapeDtypeStruct((tok, slots * width), BF16),
-        in_specs=[pl.BlockSpec(memory_space=pltpu.SMEM), vmem, vmem, hbm, hbm],
-        out_specs=vmem,
+        out_shape=jax.ShapeDtypeStruct((tok, slots, width), BF16),
+        in_specs=[smem, smem, hbm, hbm, hbm, hbm],
+        out_specs=hbm,
         scratch_shapes=[
+            pltpu.VMEM((tok, slots, width), BF16),
+            pltpu.VMEM((slots, tok, width), BF16),
+            pltpu.VMEM((3, FREQ, width), BF16),
+            pltpu.VMEM((3, 8, width), F32),
+            pltpu.VMEM((8, width // 4), F32),
+            pltpu.VMEM((8, width // 4), F32),
             pltpu.VMEM((slots + 1, peers, tok, width), BF16),
             pltpu.VMEM((CHUNKS, peers, local, cols), BF16),
             pltpu.VMEM((3, width, local), BF16),
             pltpu.VMEM((slots + 1, peers * tok, 3 * local), BF16),
             pltpu.VMEM((slots + 1, peers, tok, local), BF16),
             pltpu.VMEM((slots + 1, tok, width), BF16),
-            pltpu.VMEM((1, 3, width), F32),
             pltpu.VMEM((CHUNKS, tok, cols), BF16),
             pltpu.VMEM((CHUNKS, tok, cols), BF16),
-            dma((CHUNKS + 1,)),
+            pltpu.VMEM((slots, CHUNKS, tok, cols), BF16),
+            pltpu.VMEM((tok, slots, width), BF16),
+            dma((CHUNKS + 3,)),
             dma((n_items, 9)),
             dma((n_items, 9)),
             dma((slots + 1, peers)),
@@ -538,18 +594,20 @@
             dma((2, 5)),
             dma((2,)),
             dma((2, CHUNKS)),
+            dma((CHUNKS,)),
         ],
         compiler_params=pltpu.CompilerParams(
             collective_id=0, has_side_effects=True, vmem_limit_bytes=60 * 1024 * 1024
         ),
     )(
         target,
-        latents.reshape(tok, slots * width),
-        mods,
+        timestep,
+        latents,
+        jnp.transpose(mod_weight[0], (1, 0, 2)),
         jnp.transpose(qkv_weight[0], (1, 0, 2)),
         out_weight[0],
     )
-    return updated.reshape(tok, slots, width)
+    return updated
 
 
 def solution(mesh):

time: 119 us -> 107 us (0.90)
  Pallas kernels: 108 us -> 104 us
  local copies, waits for them, and re-layouts: 6.21 us -> 2.92 us
  other arithmetic: 2.43 us -> 0 us
  matrix products: 1.33 us -> 0 us
    pallas_call x1, Pallas kernels: 108 us -> 104 us  [kernel_body(): pl.pallas_call(functools.partial(block_kernel, sections), out_shape=jax.S...]
    reshape x1 -> x0, local copies, waits for them, and re-layouts: 2.62 us -> none  [kernel_body(): return updated.reshape(tok, slots, width)]
    unnamed x5 -> x1, local copies, waits for them, and re-layouts: 1.35 us -> 2.92 us
    dynamic_slice x1 -> x0, other arithmetic: 1.51 us -> none  [kernel_body(): own_steps = lax.dynamic_slice_in_dim(timestep, home * slots, slots)]
    dynamic_slice x1 -> x0, local copies, waits for them, and re-layouts: 1.45 us -> none  [kernel_body(): first = lax.dynamic_slice_in_dim(target, home * slots, 1) != home]
    dot_general x1 -> x0, matrix products: 1.33 us -> none  [modulate(): jnp.einsum('bf,fcd->bcd', feature, mod_table.astype(jnp.float32), precisi...]
where the time goes in v2:
time: 107 us
  Pallas kernels  104 us (97%)
  local copies, waits for them, and re-layouts  2.92 us (3%)
    pallas_call x1, Pallas kernels, kernel_body(): pl.pallas_call(functools.partial(block_kernel, sections), out_shape=jax.S...  104 us
    unnamed x1, local copies, waits for them, and re-layouts  2.92 us

profile of v2, /device:TPU:0, one launch (start us, length us, event | category | flops | bytes accessed | tf_op | source)
XLA Modules:
  0.0 106.5 jit_solution(1377384225826198007)
XLA Ops:
  0.0 103.6 %shard_map.64 = bf16[128,2,2048]{2,1,0:T(2,128)(2,1)} custom-call(s32[8]{0:T(128)} %target.1, s32[8]{0:T(128)} %timestep.1, bf16[128,2,2048]{2,1,0:T(2,128)(2,1)} %latents_hbm.1, bf16[3,256,2048]{2,1,0:T(8,128)(2,1)} %bitcast.7, bf16[3,2048,256]{2,1,0:T(8,128)(2,1)} %bitcast.8, bf16[256,2048]{1,0:T(8,128)(2,1)} %bitcast.9), custom_call_target="tpu_custom_call" | custom-call | tf_op jit(solution)/shard_map/pallas_call | solution.py:566
  103.6 2.9 %copy.8 = bf16[128,2,2048]{2,1,0:T(2,128)(2,1)} copy(bf16[128,2,2048]{2,1,0:T(2,128)(2,1)} %shard_map.64) | data formatting | bytes 2097152

commit v3 on v2

--- a/solution.py
+++ b/solution.py
@@ -120,8 +120,8 @@
     sections, target, timestep, latents_hbm, w_mod_hbm, w_qkv_hbm, w_out_hbm,
     updated_hbm,
     latents, raw, w_mod, mods, mods_out, mods_in, gathered, w_out, w_qkv, qkv, mix_send, mix_recv,
-    back, back_in, hold, updated,
-    load_sem, send_sem, recv_sem, mix_send_sem, mix_recv_sem, hand_sem, share_sem, mods_sem,
+    part, part_send, part_recv, back, back_in, hold, updated,
+    load_sem, send_sem, recv_sem, table_sem, mix_sem, part_sem, hand_sem, share_sem, mods_sem,
     back_sem, store_sem,
 ):
     tok, slots, width = latents.shape
@@ -139,19 +139,20 @@
     to_c = 1 - 2 * core
     dev_x, dev_y, dev_c = me + to_x, me + to_y, me + to_c
     diag = me + to_x + to_y
+    row = me % 4
     has_prev = section > 0
     has_next = section < sections - 1
 
     load_out = [
         pltpu.make_async_copy(
-            w_out_hbm.at[:, j * cols : (j + 1) * cols], w_out.at[j, me], load_sem.at[j]
+            w_out_hbm.at[:, j * cols : (j + 1) * cols], w_out.at[j, row], load_sem.at[j]
         )
         for j in range(CHUNKS)
     ]
     load_qkv = pltpu.make_async_copy(w_qkv_hbm, w_qkv, load_sem.at[CHUNKS])
     load_mod = pltpu.make_async_copy(w_mod_hbm, w_mod, load_sem.at[CHUNKS + 1])
     load_latents = pltpu.make_async_copy(latents_hbm, latents, load_sem.at[CHUNKS + 2])
-    for copy in (load_out[0], load_mod, load_latents, *load_out[1:], load_qkv):
+    for copy in (load_out[0], load_latents, load_mod, *load_out[1:], load_qkv):
         copy.start()
 
     barrier = pltpu.get_barrier_semaphore()
@@ -189,47 +190,71 @@
     def mask(flag, shape):
         return jnp.broadcast_to(flag, shape) != 0
 
-    def piece(item, owner, part):
-        kind, j = item
-        ref = w_out if kind == "w" else gathered
-        rows = ref.shape[2]
+    def piece(slot, owner, part):
+        rows = gathered.shape[2]
         if part is None:
-            return ref.at[j, owner]
-        return ref.at[j, owner, pl.ds(part * (rows // 2), rows // 2)]
-
-    items = [("w", 0), ("t", 0), ("t", 1)] + [("w", j) for j in range(1, CHUNKS)]
-    sends = [
-        (me, None, dev_x), (me, None, dev_y), (me, None, dev_c),
-        (dev_x, 0, dev_y), (dev_x, None, dev_c),
-        (dev_y, 1, dev_x), (dev_y, None, dev_c),
-        (diag, 0, dev_c), (diag, 1, dev_c),
-    ]
+            return gathered.at[slot, owner]
+        return gathered.at[slot, owner, pl.ds(part * (rows // 2), rows // 2)]
+
     comes = [
         dev_x, dev_y, dev_c, diag, dev_x + to_c, diag, dev_y + to_c, diag + to_c, diag + to_c,
+        dev_y,
     ]
 
+    def route(n, kind):
+        return [
+            (me, None, dev_x), (me, 0, dev_y), (me, None, dev_c),
+            (dev_x, 0, dev_y), (dev_x, None, dev_c),
+            (dev_x, 1, dev_y), (dev_y, None, dev_c),
+            (diag, 0, dev_c), (diag, 1, dev_c), (me, 1, dev_y),
+        ][kind]
+
     def send(n, kind):
-        owner, part, target = sends[kind]
-        ref = piece(items[n], owner, part)
+        owner, part, target = route(n, kind)
+        ref = piece(n, owner, part)
         return pltpu.make_async_remote_copy(
             ref, ref, send_sem.at[n, kind], recv_sem.at[n, kind],
             device_id=(section, target), device_id_type=MESH,
         )
 
     def arrive(n, kind):
-        _, part, target = sends[kind]
-        ref = piece(items[n], comes[kind], part)
+        _, part, target = route(n, kind)
+        ref = piece(n, comes[kind], part)
         pltpu.make_async_remote_copy(
             ref, ref, send_sem.at[n, kind], recv_sem.at[n, kind],
             device_id=(section, target), device_id_type=MESH,
         ).wait_recv()
 
+    def table_copy(j, kind, shift):
+        owner, target = [(me, dev_x), (me, dev_c), (dev_x, dev_c)][kind]
+        ref = w_out.at[j, (owner + shift) % 4]
+        return pltpu.make_async_remote_copy(
+            ref, ref, table_sem.at[0, j, kind], table_sem.at[1, j, kind],
+            device_id=(section, target), device_id_type=MESH,
+        )
+
+    def table_begin(*js):
+        for j in js:
+            load_out[j].wait()
+            table_copy(j, 0, 0).start()
+            table_copy(j, 1, 0).start()
+
+    def table_forward(*js):
+        for j in js:
+            table_copy(j, 0, to_x).wait_recv()
+            table_copy(j, 2, 0).start()
+
+    def table_arrive(*js):
+        for j in js:
+            table_copy(j, 1, to_c).wait_recv()
+            table_copy(j, 2, to_c).wait_recv()
+
     handed = [(me, None), (dev_x, None), (dev_y, None), (diag, 0), (diag, 1)]
 
     def hand_copy(k):
         owner, part = handed[k]
         return pltpu.make_async_remote_copy(
-            piece(("t", 0), owner, part), piece(("t", 2), owner, part),
+            piece(0, owner, part), piece(2, owner, part),
             hand_sem.at[0, k], hand_sem.at[1, k],
             device_id=(section + 1, me), device_id_type=MESH,
         )
@@ -241,7 +266,7 @@
 
     def share_copy(k, shift):
         owner, part = handed[k]
-        ref = piece(("t", 2), owner + shift, part)
+        ref = piece(2, owner + shift, part)
         return pltpu.make_async_remote_copy(
             ref, ref, share_sem.at[0, k], share_sem.at[1, k],
             device_id=(section, dev_c), device_id_type=MESH,
@@ -329,41 +354,43 @@
 
         lax.fori_loop(0, tok // 16, rows16, 0)
 
-    def begin(n):
-        kind, j = items[n]
-        if kind == "w":
-            load_out[j].wait()
-        for kind_sent in (0, 1, 2):
-            send(n, kind_sent).start()
-
-    def forward(n):
+    def begin(n, *kinds):
+        for kind in kinds:
+            send(n, kind).start()
+
+    def forward_x(n):
         arrive(n, 0)
         send(n, 3).start()
+        send(n, 5).start()
         send(n, 4).start()
-        if n == t0:
+        if n == 0:
             hand(1)
+
+    def forward_y(n):
         arrive(n, 1)
-        send(n, 5).start()
+        arrive(n, 9)
         send(n, 6).start()
-        if n == t0:
+        if n == 0:
             hand(2)
 
     def last_forward(n):
         arrive(n, 3)
         send(n, 7).start()
-        if n == t0:
+        if n == 0:
             hand(3)
         arrive(n, 5)
         send(n, 8).start()
-        if n == t0:
+        if n == 0:
             hand(4)
 
-    def mix_copy(slot, step, owner, target):
-        return pltpu.make_async_remote_copy(
-            mix_send.at[slot, target],
-            mix_recv.at[slot, :, pl.ds(pl.multiple_of(owner * local, local), local)],
-            mix_send_sem.at[slot, step], mix_recv_sem.at[slot, step],
-            device_id=(section, target), device_id_type=MESH,
+    mix_targets = [dev_x, dev_x + to_c, dev_c]
+
+    def mix_copy(slot, k, owner):
+        return pltpu.make_async_remote_copy(
+            mix_send.at[slot, mix_targets[k] % 4],
+            mix_recv.at[slot, :, pl.ds(pl.multiple_of(owner % 4 * local, local), local)],
+            mix_sem.at[0, slot, k], mix_sem.at[1, slot, k],
+            device_id=(section, mix_targets[k]), device_id_type=MESH,
         )
 
     def project(slot, first, end):
@@ -380,8 +407,10 @@
         lax.fori_loop(first, end, step, 0)
 
     def queries(slot, first, end):
-        def step(i, _):
-            rows = pl.ds(pl.multiple_of(i * 2 * tok, 2 * tok), 2 * tok)
+        def step(k, _):
+            chip_x = (x + 1 + k // 2) % 2
+            chip_y = k % 2
+            rows = pl.ds(pl.multiple_of((chip_y * 2 + chip_x) * 2 * tok, 2 * tok), 2 * tok)
             for h in range(heads):
                 a = h * HEAD_DIM
                 query = qkv[slot, rows, a : a + HEAD_DIM]
@@ -394,28 +423,43 @@
                 probs = jnp.exp((scores - top) * HEAD_DIM ** (-0.5))
                 total = jnp.sum(probs, axis=-1, keepdims=True)
                 mixed = jnp.dot(probs.astype(BF16), vals, preferred_element_type=F32) / total
-                mix_send[slot, pl.ds(2 * i, 2), :, a : a + HEAD_DIM] = mixed.astype(
-                    BF16
-                ).reshape(2, tok, HEAD_DIM)
+                mixed = mixed.astype(BF16).reshape(2, tok, HEAD_DIM)
+                at = pl.ds(pl.multiple_of(chip_y * tok, tok), tok)
+                mix_send[slot, pl.ds(2 * chip_x, 2), at, a : a + HEAD_DIM] = mixed
             return 0
 
         lax.fori_loop(first, end, step, 0)
 
-    def exchange(slot):
-        mix_recv[slot, :, pl.ds(pl.multiple_of(me * local, local), local)] = mix_send[slot, me]
-        for step in range(1, peers):
-            mix_copy(slot, step, me, (me + step) % peers).start()
+    def mix(slot, *ks):
+        for k in ks:
+            mix_copy(slot, k, me).start()
+        if 2 in ks:
+            mix_recv[slot, :, pl.ds(pl.multiple_of(row * local, local), local)] = mix_send[slot, row]
 
     def mix_arrive(slot):
-        for step in range(1, peers):
-            mix_copy(slot, step, (me + peers - step) % peers, (me + step) % peers).wait_recv()
+        for k in range(3):
+            mix_copy(slot, k, mix_targets[k]).wait_recv()
+
+    def part_copy(slot, j):
+        return pltpu.make_async_remote_copy(
+            part_send.at[slot, j], part_recv.at[slot, j],
+            part_sem.at[0, slot, j], part_sem.at[1, slot, j],
+            device_id=(section, dev_y), device_id_type=MESH,
+        )
 
     def project_out(slot, j):
-        table = w_out[j].reshape(peers * local, cols)
+        table = w_out[j].reshape(4 * local, cols)
+        theirs = mix_recv[slot, pl.ds(pl.multiple_of((1 - y) * tok, tok), tok), :]
+        part_send[slot, j] = jnp.dot(theirs, table, preferred_element_type=F32).astype(BF16)
+        part_copy(slot, j).start()
+        ours = mix_recv[slot, pl.ds(pl.multiple_of(y * tok, tok), tok), :]
+        part[slot, j] = jnp.dot(ours, table, preferred_element_type=F32)
+
+    def combine(slot, j):
+        part_copy(slot, j).wait_recv()
         at = slice(j * cols, (j + 1) * cols)
-        change = mods[2, slot : slot + 1, at] * jnp.dot(
-            mix_recv[slot], table, preferred_element_type=F32
-        )
+        proj = part[slot, j] + part_recv[slot, j].astype(F32)
+        change = mods[2, slot : slot + 1, at] * proj
         if slot == 2:
             back[j] = change.astype(BF16)
 
@@ -449,84 +493,93 @@
             updated[rows, 1, at] = jnp.where(pick, second, first)
         store_copy(j).start()
 
-    half = peers // 4
-    w0, t0, t1, w1, w2, w3 = range(len(items))
-    begin(w0)
+    everything = range(CHUNKS)
+    early, late = everything[: CHUNKS // 2], everything[CHUNKS // 2 :]
+    table_begin(0)
     modulation()
     load_latents.wait()
     unpack()
+    norm(1)
+    begin(1, 1, 2)
 
     @pl.when(has_next)
     def _():
         mods_copy().wait_recv()
 
     norm(0)
-    begin(t0)
+    begin(0, 0, 1, 9, 2)
     hand(0)
-    begin(w1)
-    norm(1)
-    forward(w0)
+    begin(1, 0)
+    table_begin(*early[1:])
     load_qkv.wait()
-    arrive(t0, 2)
+    arrive(0, 2)
     project(0, 0, 1)
-    forward(t0)
-    begin(t1)
+    arrive(1, 2)
+    project(1, 0, 1)
+    forward_x(0)
+    forward_y(0)
+    begin(1, 9)
     for kind in (4, 6):
-        arrive(t0, kind)
+        arrive(0, kind)
     project(0, 1, 3)
     share(0)
-    last_forward(w0)
-    forward(w1)
-    last_forward(t0)
+    forward_x(1)
+    last_forward(0)
     for kind in (7, 8):
-        arrive(t0, kind)
+        arrive(0, kind)
     project(0, 3, 4)
-    begin(w2)
-    queries(0, 0, half)
-    last_forward(w1)
-    queries(0, half, 2 * half)
-    exchange(0)
+    queries(0, 0, 2)
+    mix(0, 0, 1)
+    table_begin(*late)
     share(1)
+    table_forward(*early[: len(early) // 2])
+    queries(0, 2, 4)
+    mix(0, 2)
     shared(0, 1)
     project(2, 0, 2)
-    forward(t1)
-    begin(w3)
-    for kind in (2, 4, 6):
-        arrive(t1, kind)
-    project(1, 0, 3)
+    table_forward(*early[len(early) // 2 :])
+    forward_y(1)
     share(2)
-    forward(w2)
-    last_forward(t1)
+    arrive(1, 4)
+    arrive(1, 6)
+    project(1, 1, 3)
+    mix_arrive(0)
+    for j in early:
+        table_arrive(j)
+        project_out(0, j)
+    table_forward(*late[: len(late) // 2])
+    last_forward(1)
     share(3, 4)
+    for kind in (7, 8):
+        arrive(1, kind)
+    project(1, 3, 4)
     shared(2, 3, 4)
     project(2, 2, 4)
-    queries(2, 0, half)
-    last_forward(w2)
-    forward(w3)
-    queries(2, half, 2 * half)
-    exchange(2)
-    for kind in (7, 8):
-        arrive(t1, kind)
-    project(1, 3, 4)
-    last_forward(w3)
-    queries(1, 0, half)
+    queries(2, 0, 2)
+    mix(2, 0, 1)
+    table_forward(*late[len(late) // 2 :])
+    for j in late:
+        table_arrive(j)
+        project_out(0, j)
+    queries(2, 2, 4)
+    mix(2, 2)
+    queries(1, 0, 2)
+    mix(1, 0, 1)
     mix_arrive(2)
-    for n, j in ((w0, 0), (w1, 1)):
-        for kind in (2, 4, 6, 7, 8):
-            arrive(n, kind)
+    for j in everything:
         project_out(2, j)
-    queries(1, half, 2 * half)
-    exchange(1)
-    for n, j in ((w2, 2), (w3, 3)):
-        for kind in (2, 4, 6, 7, 8):
-            arrive(n, kind)
-        project_out(2, j)
-    mix_arrive(0)
-    for j in range(CHUNKS):
-        project_out(0, j)
+    queries(1, 2, 4)
+    mix(1, 2)
+    for j in everything:
+        combine(0, j)
     mix_arrive(1)
-    for j in range(CHUNKS):
+    for j in everything:
         project_out(1, j)
+    for j in everything:
+        combine(2, j)
+    for j in everything:
+        combine(1, j)
+    for j in everything:
         write(j)
     for j in range(CHUNKS):
         store_copy(j).wait()
@@ -546,12 +599,17 @@
         for k in range(len(handed)):
             share_copy(k, 0).wait_send()
 
-    for n in range(len(items)):
-        for kind in range(len(sends)):
+    for n in range(slots):
+        for kind in range(len(comes)):
             send(n, kind).wait_send()
-    for slot in range(3):
-        for step in range(1, peers):
-            mix_copy(slot, step, me, (me + step) % peers).wait_send()
+    for j in everything:
+        for kind in range(3):
+            table_copy(j, kind, 0).wait_send()
+    for slot in range(slots + 1):
+        for k in range(3):
+            mix_copy(slot, k, me).wait_send()
+        for j in everything:
+            part_copy(slot, j).wait_send()
 
 
 def kernel_body(sections, latents, timestep, target, qkv_weight, mod_weight, out_weight):
@@ -561,7 +619,6 @@
     smem = pl.BlockSpec(memory_space=pltpu.SMEM)
     hbm = pl.BlockSpec(memory_space=pl.ANY)
     cols = width // CHUNKS
-    n_items = slots + CHUNKS
     dma = pltpu.SemaphoreType.DMA
     updated = pl.pallas_call(
         functools.partial(block_kernel, sections),
@@ -576,20 +633,24 @@
             pltpu.VMEM((8, width // 4), F32),
             pltpu.VMEM((8, width // 4), F32),
             pltpu.VMEM((slots + 1, peers, tok, width), BF16),
-            pltpu.VMEM((CHUNKS, peers, local, cols), BF16),
+            pltpu.VMEM((CHUNKS, 4, local, cols), BF16),
             pltpu.VMEM((3, width, local), BF16),
             pltpu.VMEM((slots + 1, peers * tok, 3 * local), BF16),
-            pltpu.VMEM((slots + 1, peers, tok, local), BF16),
-            pltpu.VMEM((slots + 1, tok, width), BF16),
+            pltpu.VMEM((slots + 1, 4, 2 * tok, local), BF16),
+            pltpu.VMEM((slots + 1, 2 * tok, 4 * local), BF16),
+            pltpu.VMEM((slots + 1, CHUNKS, tok, cols), F32),
+            pltpu.VMEM((slots + 1, CHUNKS, tok, cols), BF16),
+            pltpu.VMEM((slots + 1, CHUNKS, tok, cols), BF16),
             pltpu.VMEM((CHUNKS, tok, cols), BF16),
             pltpu.VMEM((CHUNKS, tok, cols), BF16),
             pltpu.VMEM((slots, CHUNKS, tok, cols), BF16),
             pltpu.VMEM((tok, slots, width), BF16),
             dma((CHUNKS + 3,)),
-            dma((n_items, 9)),
-            dma((n_items, 9)),
-            dma((slots + 1, peers)),
-            dma((slots + 1, peers)),
+            dma((slots, 10)),
+            dma((slots, 10)),
+            dma((2, CHUNKS, 3)),
+            dma((2, slots + 1, 3)),
+            dma((2, slots + 1, CHUNKS)),
             dma((2, 5)),
             dma((2, 5)),
             dma((2,)),

time: 107 us -> 101 us (0.944)
  Pallas kernels: 104 us -> 97.5 us
    pallas_call x1, Pallas kernels: 104 us -> 97.5 us  [kernel_body(): pl.pallas_call(functools.partial(block_kernel, sections), out_shape=jax.S...]
where the time goes in v3:
time: 101 us; the launch traced here: 100 us
  Pallas kernels  97.5 us (97%)
  local copies, waits for them, and re-layouts  2.92 us (3%)
    pallas_call x1, Pallas kernels, kernel_body(): pl.pallas_call(functools.partial(block_kernel, sections), out_shape=jax.S...  97.5 us
    unnamed x1, local copies, waits for them, and re-layouts  2.92 us

profile of v3, /device:TPU:0, one launch (start us, length us, event | category | flops | bytes accessed | tf_op | source)
XLA Modules:
  0.0 100.4 jit_solution(13917956156721930827)
XLA Ops:
  0.0 97.5 %shard_map.64 = bf16[128,2,2048]{2,1,0:T(2,128)(2,1)} custom-call(s32[8]{0:T(128)} %target.1, s32[8]{0:T(128)} %timestep.1, bf16[128,2,2048]{2,1,0:T(2,128)(2,1)} %latents_hbm.1, bf16[3,256,2048]{2,1,0:T(8,128)(2,1)} %bitcast.7, bf16[3,2048,256]{2,1,0:T(8,128)(2,1)} %bitcast.8, bf16[256,2048]{1,0:T(8,128)(2,1)} %bitcast.9), custom_call_target="tpu_custom_call" | custom-call | tf_op jit(solution)/shard_map/pallas_call | solution.py:623
  97.5 2.9 %copy.8 = bf16[128,2,2048]{2,1,0:T(2,128)(2,1)} copy(bf16[128,2,2048]{2,1,0:T(2,128)(2,1)} %shard_map.64) | data formatting | bytes 2097152

commit v4 on v3

--- a/solution.py
+++ b/solution.py
@@ -470,11 +470,9 @@
             return
         hold[slot, j] = (raw[slot, :, at].astype(F32) + change).astype(BF16)
 
-    def store_copy(j):
-        at = slice(j * cols, (j + 1) * cols)
-        return pltpu.make_async_copy(
-            updated.at[:, :, at], updated_hbm.at[:, :, at], store_sem.at[j]
-        )
+    def store_copy(slot, j):
+        at = slice(slot * width + j * cols, slot * width + (j + 1) * cols)
+        return pltpu.make_async_copy(updated.at[:, at], updated_hbm.at[:, at], store_sem.at[slot, j])
 
     def write(j):
         @pl.when(has_next)
@@ -489,9 +487,12 @@
             returned = raw[0, rows, at].astype(F32) + back_in[j, rows, :].astype(F32)
             first = jnp.where(moved, returned.astype(BF16), hold[0, j, rows, :])
             second = hold[1, j, rows, :]
-            updated[rows, 0, at] = jnp.where(pick, first, second)
-            updated[rows, 1, at] = jnp.where(pick, second, first)
-        store_copy(j).start()
+            updated[rows, at] = jnp.where(pick, first, second)
+            updated[rows, slice(width + at.start, width + at.stop)] = jnp.where(
+                pick, second, first
+            )
+        for slot in range(slots):
+            store_copy(slot, j).start()
 
     everything = range(CHUNKS)
     early, late = everything[: CHUNKS // 2], everything[CHUNKS // 2 :]
@@ -547,22 +548,25 @@
     for j in early:
         table_arrive(j)
         project_out(0, j)
-    table_forward(*late[: len(late) // 2])
     last_forward(1)
+    table_forward(2)
     share(3, 4)
-    for kind in (7, 8):
-        arrive(1, kind)
-    project(1, 3, 4)
     shared(2, 3, 4)
     project(2, 2, 4)
     queries(2, 0, 2)
     mix(2, 0, 1)
-    table_forward(*late[len(late) // 2 :])
-    for j in late:
+    for j in (2,):
         table_arrive(j)
         project_out(0, j)
+    table_forward(3)
     queries(2, 2, 4)
     mix(2, 2)
+    for kind in (7, 8):
+        arrive(1, kind)
+    project(1, 3, 4)
+    for j in (3,):
+        table_arrive(j)
+        project_out(0, j)
     queries(1, 0, 2)
     mix(1, 0, 1)
     mix_arrive(2)
@@ -582,7 +586,8 @@
     for j in everything:
         write(j)
     for j in range(CHUNKS):
-        store_copy(j).wait()
+        for slot in range(slots):
+            store_copy(slot, j).wait()
 
         @pl.when(has_prev)
         def _():
@@ -612,6 +617,12 @@
             part_copy(slot, j).wait_send()
 
 
+def spread_kernel(flat, spread):
+    _, slots, width = spread.shape
+    for slot in range(slots):
+        spread[:, slot, :] = flat[:, slot * width : (slot + 1) * width]
+
+
 def kernel_body(sections, latents, timestep, target, qkv_weight, mod_weight, out_weight):
     tok, slots, width = latents.shape
     local = out_weight.shape[1]
@@ -622,7 +633,7 @@
     dma = pltpu.SemaphoreType.DMA
     updated = pl.pallas_call(
         functools.partial(block_kernel, sections),
-        out_shape=jax.ShapeDtypeStruct((tok, slots, width), BF16),
+        out_shape=jax.ShapeDtypeStruct((tok, slots * width), BF16),
         in_specs=[smem, smem, hbm, hbm, hbm, hbm],
         out_specs=hbm,
         scratch_shapes=[
@@ -644,7 +655,7 @@
             pltpu.VMEM((CHUNKS, tok, cols), BF16),
             pltpu.VMEM((CHUNKS, tok, cols), BF16),
             pltpu.VMEM((slots, CHUNKS, tok, cols), BF16),
-            pltpu.VMEM((tok, slots, width), BF16),
+            pltpu.VMEM((tok, slots * width), BF16),
             dma((CHUNKS + 3,)),
             dma((slots, 10)),
             dma((slots, 10)),
@@ -655,7 +666,7 @@
             dma((2, 5)),
             dma((2,)),
             dma((2, CHUNKS)),
-            dma((CHUNKS,)),
+            dma((slots, CHUNKS)),
         ],
         compiler_params=pltpu.CompilerParams(
             collective_id=0, has_side_effects=True, vmem_limit_bytes=60 * 1024 * 1024
@@ -668,7 +679,14 @@
         jnp.transpose(qkv_weight[0], (1, 0, 2)),
         out_weight[0],
     )
-    return updated
+    blocks = 1
+    return pl.pallas_call(
+        spread_kernel,
+        grid=(blocks,),
+        out_shape=jax.ShapeDtypeStruct((tok, slots, width), BF16),
+        in_specs=[pl.BlockSpec((tok // blocks, slots * width), lambda i: (i, 0))],
+        out_specs=pl.BlockSpec((tok // blocks, slots, width), lambda i: (i, 0, 0)),
+    )(updated)
 
 
 def solution(mesh):

time: 101 us -> 99.4 us (0.984)
  local copies, waits for them, and re-layouts: 2.92 us -> 0 us
  Pallas kernels: 97.5 us -> 99 us
    unnamed x1 -> x0, local copies, waits for them, and re-layouts: 2.92 us -> none
    pallas_call x0 -> x1, Pallas kernels: none -> 2.65 us  [kernel_body(): pl.pallas_call(spread_kernel, grid=(blocks,), out_shape=jax.ShapeDtypeStr...]
    pallas_call x1, Pallas kernels: 97.5 us -> 96.4 us  [kernel_body(): pl.pallas_call(functools.partial(block_kernel, sections), out_shape=jax.S...]
where the time goes in v4:
time: 99.4 us; the launch traced here: 99 us
  Pallas kernels  99 us (100%)
    pallas_call x1, Pallas kernels, kernel_body(): pl.pallas_call(functools.partial(block_kernel, sections), out_shape=jax.S...  96.4 us
    pallas_call x1, Pallas kernels, kernel_body(): pl.pallas_call(spread_kernel, grid=(blocks,), out_shape=jax.ShapeDtypeStr...  2.65 us

profile of v4, /device:TPU:0, one launch (start us, length us, event | category | flops | bytes accessed | tf_op | source)
XLA Modules:
  0.0 99.0 jit_solution(11819071737472956463)
XLA Ops:
  0.0 96.4 %shard_map.64.flat = bf16[128,4096]{1,0:T(8,128)(2,1)} custom-call(s32[8]{0:T(128)} %target.1, s32[8]{0:T(128)} %timestep.1, bf16[128,2,2048]{2,1,0:T(2,128)(2,1)} %latents_hbm.1, bf16[3,256,2048]{2,1,0:T(8,128)(2,1)} %bitcast.7, bf16[3,2048,256]{2,1,0:T(8,128)(2,1)} %bitcast.8, bf16[256,2048]{1,0:T(8,128)(2,1)} %bitcast.9), custom_call_target="tpu_custom_call" | custom-call | tf_op jit(solution)/shard_map/pallas_call | solution.py:634
  96.4 2.6 %shard_map.65 = bf16[128,2,2048]{2,1,0:T(2,128)(2,1)} custom-call(bf16[128,4096]{1,0:T(8,128)(2,1)} %shard_map.64.flat), custom_call_target="tpu_custom_call" | custom-call | tf_op jit(solution)/shard_map/pallas_call | solution.py:683
